TPU v7x, 32 devices: a whole 2x2x4 slice. The times are simulated.
32 devices in a mesh: row: 8 (over z, core), col: 4 (over y, x).
Axes of the slice: x: 2, y: 2, z: 4, core: 2. Of those that a mesh axis runs over, the one named last changes fastest.
Arguments:
- genotypes: int32 [512, 16384], P(('row', 'col')), may hold values from 0 to 2, as said below
- snp_index: int32 [512], P(('row', 'col')), may hold values from 0 to 2047, as said below
- freq_table: float32 [2048], replicated, as said below
- prior: float32 [16384, 16384], P('row', 'col'), as said below
- start_vectors: float32 [16384, 20], P('row'), may hold values from -6 to 6
Outputs:
- grm: float32 [16384, 16384], P('row', 'col')
- pcs: float32 [16384, 20], P('col')
- spectrum: float32 [3, 20], replicated
Inputs may be any that keep to these rules, and one draw needn't show every extreme that they name: `genotypes`: genotype dosages 0, 1 or 2. `snp_index`: strictly increasing; entry j lies in 4 * j to 4 * j + 3. `freq_table`: frequencies are multiples of 1/1024 between 52/1024 and 512/1024. `prior`: exactly symmetric; diagonal between 1 and 2, off-diagonal entries small.
All inputs are finite; a program needn't handle non-finite values.
Results may differ from a plain program's by a relative error of at most 0.0075.
Values may be sent and summed in bfloat16 or wider, within the bound.
A program may use at most 128 MiB of HBM per device.

v0:
```python
import functools

import jax
import jax.numpy as jnp
from jax import lax
from jax.experimental import pallas as pl
from jax.experimental.pallas import tpu as pltpu
from jax.sharding import PartitionSpec as P

ITERS = 3
MESH = pl.DeviceIdType.MESH


def standardize(genotypes, allele_freq):
    doubled = 2.0 * allele_freq
    spread = jnp.sqrt(doubled * (1.0 - allele_freq))
    return (genotypes.astype(jnp.float32) - doubled[:, None]) / spread[:, None]


def panel_kernel(nr, nc, std_ref, rp_ref, cp_ref, s1, r1, s2, r2, s3, r3, sr, rr, sl, rl):
    row, col = lax.axis_index("row"), lax.axis_index("col")
    lr, lc = rp_ref.shape[3], cp_ref.shape[3]
    row_peers = [lax.rem(row + d, nr) for d in range(1, nr)]
    col_peers = [lax.rem(col + d, nc) for d in range(1, nc)]

    barrier = pltpu.get_barrier_semaphore()
    for peer in row_peers:
        pl.semaphore_signal(barrier, inc=1, device_id={"row": peer}, device_id_type=MESH)
    for peer in col_peers:
        pl.semaphore_signal(barrier, inc=1, device_id={"col": peer}, device_id_type=MESH)
    pl.semaphore_wait(barrier, nr + nc - 2)

    def remote(src, dst, send_sem, recv_sem, target):
        return pltpu.make_async_remote_copy(
            src_ref=src,
            dst_ref=dst,
            send_sem=send_sem,
            recv_sem=recv_sem,
            device_id=target,
            device_id_type=MESH,
        )

    def samples(index, length):
        return std_ref.at[:, pl.ds(pl.multiple_of(index * length, 128), length)]

    by_col, by_row, across = [], [], []
    for d, peer in enumerate(col_peers):
        by_col.append(
            remote(samples(peer, lc), cp_ref.at[row, col], s2.at[d], r2.at[d], {"col": peer})
        )
        by_col[-1].start()
    for d, peer in enumerate(row_peers):
        by_row.append(
            remote(samples(peer, lr), rp_ref.at[row, col], s1.at[d], r1.at[d], {"row": peer})
        )
        by_row[-1].start()
    cp_ref[row, col] = samples(col, lc)[...]
    rp_ref[row, col] = samples(row, lr)[...]

    right, left = lax.rem(row + 1, nr), lax.rem(row + nr - 1, nr)

    def rightward(s):
        chunk = cp_ref.at[lax.rem(row - s + nr, nr)]
        return remote(chunk, chunk, sr.at[s], rr.at[s], {"row": right})

    def leftward(s):
        chunk = cp_ref.at[lax.rem(row + s, nr)]
        return remote(chunk, chunk, sl.at[s], rl.at[s], {"row": left})

    def sends(s):
        return (row >= s) & (row < nr - 1), (row + s < nr) & (row > 0)

    def start(s):
        to_right, to_left = sends(s)

        @pl.when(to_right)
        def _():
            rightward(s).start()

        @pl.when(to_left)
        def _():
            leftward(s).start()

    def receive(s):
        @pl.when(row - 1 - s >= 0)
        def _():
            chunk = cp_ref.at[lax.rem(row - 1 - s + nr, nr)]
            remote(chunk, chunk, sr.at[s], rr.at[s], {"row": right}).wait_recv()

        @pl.when(row + 1 + s < nr)
        def _():
            chunk = cp_ref.at[lax.rem(row + 1 + s, nr)]
            remote(chunk, chunk, sl.at[s], rl.at[s], {"row": left}).wait_recv()

    for copy in by_col:
        copy.wait_recv()
    for s in range(nr - 1):
        start(s)
        if s == min(1, nr - 2):
            for copy in by_row:
                copy.wait_recv()
            for d, peer in enumerate(col_peers):
                piece = rp_ref.at[:, col]
                across.append(remote(piece, piece, s3.at[d], r3.at[d], {"col": peer}))
                across[-1].start()
        receive(s)
    for copy in across:
        copy.wait_recv()
    for copy in by_col + by_row + across:
        copy.wait_send()
    for s in range(nr - 1):
        to_right, to_left = sends(s)

        @pl.when(to_right)
        def _():
            rightward(s).wait_send()

        @pl.when(to_left)
        def _():
            leftward(s).wait_send()


def make_panels(standard):
    nr, nc = lax.axis_size("row"), lax.axis_size("col")
    own, samples = standard.shape
    dma = pltpu.SemaphoreType.DMA
    vmem = pl.BlockSpec(memory_space=pltpu.VMEM)
    panels = pl.pallas_call(
        functools.partial(panel_kernel, nr, nc),
        in_specs=[vmem],
        out_specs=[vmem] * 2,
        out_shape=[
            jax.ShapeDtypeStruct((nr, nc, own, samples // nr), jnp.bfloat16),
            jax.ShapeDtypeStruct((nr, nc, own, samples // nc), jnp.bfloat16),
        ],
        scratch_shapes=[dma((nr - 1,))] * 2
        + [dma((nc - 1,))] * 4
        + [dma((nr - 1,))] * 4,
        compiler_params=pltpu.CompilerParams(
            collective_id=20, has_side_effects=True, vmem_limit_bytes=56 * 2**20
        ),
        name="panels",
    )(standard)
    return [panel.reshape(nr * nc * own, panel.shape[3]) for panel in panels]


def tile_kernel(scale, step, rows_ref, cols_ref, start_ref, prior_ref, grm_ref, short_ref, first_ref, turned):
    @pl.when(pl.program_id(0) == 0)
    def _():
        turned[...] = rows_ref[...].T

    first = jnp.zeros(first_ref.shape, jnp.float32)
    for low in range(0, prior_ref.shape[0], step):
        part = slice(low, low + step)
        window = jnp.dot(turned[part, :], cols_ref[...], preferred_element_type=jnp.float32)
        grm = prior_ref[part, :] + window * scale
        grm_ref[part, :] = grm
        short = grm.astype(jnp.bfloat16)
        short_ref[part, :] = short
        first = first + jnp.dot(start_ref[:, part], short, preferred_element_type=jnp.float32)
    first_ref[...] = first.astype(jnp.bfloat16)


def make_tile(row_panel, col_panel, start, prior):
    depth = row_panel.shape[0]
    rows, cols = prior.shape
    height = start.shape[0]
    bn = min(256 if depth > 1024 else 512, cols)
    return pl.pallas_call(
        functools.partial(tile_kernel, 1.0 / depth, min(512, rows)),
        grid=(cols // bn,),
        in_specs=[
            pl.BlockSpec((depth, rows), lambda j: (0, 0)),
            pl.BlockSpec((depth, bn), lambda j: (0, j)),
            pl.BlockSpec((height, rows), lambda j: (0, 0)),
            pl.BlockSpec((rows, bn), lambda j: (0, j)),
        ],
        out_specs=[
            pl.BlockSpec((rows, bn), lambda j: (0, j)),
            pl.BlockSpec((rows, bn), lambda j: (0, j)),
            pl.BlockSpec((height, bn), lambda j: (0, j)),
        ],
        out_shape=[
            jax.ShapeDtypeStruct((rows, cols), jnp.float32),
            jax.ShapeDtypeStruct((rows, cols), jnp.bfloat16),
            jax.ShapeDtypeStruct((height, cols), jnp.bfloat16),
        ],
        scratch_shapes=[pltpu.VMEM((rows, depth), jnp.bfloat16)],
        compiler_params=pltpu.CompilerParams(
            dimension_semantics=("arbitrary",), vmem_limit_bytes=56 * 2**20
        ),
        cost_estimate=pl.CostEstimate(
            flops=2 * rows * cols * depth, bytes_accessed=10 * rows * cols, transcendentals=0
        ),
        name="tile",
    )(row_panel, col_panel, start, prior)


def sum_kernel(axis, n, with_block, with_gram, *refs):
    refs = list(refs)
    x_ref = refs.pop(0) if with_block else None
    g_ref = refs.pop(0) if with_gram else None
    y_ref = refs.pop(0) if with_block else None
    h_ref = refs.pop(0) if with_gram else None
    if with_block:
        parts, own, land, s1, r1, s2, r2 = refs[:7]
        refs = refs[7:]
    if with_gram:
        grams, s3, r3 = refs
    me = lax.axis_index(axis)
    peers = [lax.rem(me + d, n) for d in range(1, n)]

    barrier = pltpu.get_barrier_semaphore()
    for peer in peers:
        pl.semaphore_signal(barrier, inc=1, device_id={axis: peer}, device_id_type=MESH)
    pl.semaphore_wait(barrier, n - 1)

    def send(src, dst, send_sem, recv_sem, peer):
        copy = pltpu.make_async_remote_copy(
            src_ref=src,
            dst_ref=dst,
            send_sem=send_sem,
            recv_sem=recv_sem,
            device_id={axis: peer},
            device_id_type=MESH,
        )
        copy.start()
        return copy

    first, second, third = [], [], []
    if with_block:
        for d, peer in enumerate(peers):
            first.append(send(x_ref.at[peer], parts.at[d], s1.at[d], r1.at[d], peer))
    if with_gram:
        for d, peer in enumerate(peers):
            third.append(send(g_ref, grams.at[me], s3.at[d], r3.at[d], peer))
        grams[me] = g_ref[...]
    if with_block:
        total = x_ref[me].astype(jnp.float32)
        for d, copy in enumerate(first):
            copy.wait_recv()
            total = total + parts[d].astype(jnp.float32)
        own[...] = total.astype(jnp.bfloat16)
        for d, peer in enumerate(peers):
            second.append(send(own, land.at[me], s2.at[d], r2.at[d], peer))
        land[me] = total.astype(jnp.bfloat16)
    if with_gram:
        for copy in third:
            copy.wait_recv()
        gram = grams[0]
        for j in range(1, n):
            gram = gram + grams[j]
        h_ref[...] = gram
    if with_block:
        for copy in second:
            copy.wait_recv()
        length = land.shape[2]
        for j in range(n):
            y_ref[:, j * length : (j + 1) * length] = land[j]
    for copy in first + second + third:
        copy.wait_send()


def axis_sum(axis, ident, block=None, gram=None):
    n = lax.axis_size(axis)
    dma = pltpu.SemaphoreType.DMA
    args, outs, scratch = [], [], []
    if block is not None:
        height, width = block.shape
        length = width // n
        args.append(block.reshape(height, n, length).transpose(1, 0, 2))
        outs.append(jax.ShapeDtypeStruct((height, width), jnp.bfloat16))
        scratch += [
            pltpu.VMEM((n - 1, height, length), jnp.bfloat16),
            pltpu.VMEM((height, length), jnp.bfloat16),
            pltpu.VMEM((n, height, length), jnp.bfloat16),
        ] + [dma((n - 1,))] * 4
    if gram is not None:
        args.append(gram)
        outs.append(jax.ShapeDtypeStruct(gram.shape, jnp.float32))
        scratch += [pltpu.VMEM((n,) + gram.shape, jnp.float32)] + [dma((n - 1,))] * 2
    vmem = pl.BlockSpec(memory_space=pltpu.VMEM)
    return pl.pallas_call(
        functools.partial(sum_kernel, axis, n, block is not None, gram is not None),
        in_specs=[vmem] * len(args),
        out_specs=[vmem] * len(outs),
        out_shape=outs,
        scratch_shapes=scratch,
        compiler_params=pltpu.CompilerParams(collective_id=ident, has_side_effects=True),
        name="sum" + str(ident),
    )(*args)


def factor_kernel(count, gain, gram_ref, block_ref, out_ref, diag_ref):
    height = gram_ref.shape[0]
    row = lax.broadcasted_iota(jnp.int32, (height, height), 0)
    col = lax.broadcasted_iota(jnp.int32, (height, height), 1)
    gram = gram_ref[...]
    inverse = jnp.where(row == col, 1.0, 0.0).astype(jnp.float32)
    diag = jnp.zeros((height, height), jnp.float32)
    for k in range(count):
        pivot = gram[k : k + 1, k : k + 1]
        root = jnp.sqrt(pivot)
        diag = jnp.where((row == 0) & (col == k), root, diag)
        head = gram[k : k + 1, :] / root
        tail = inverse[k : k + 1, :] / root
        below = jnp.where(row[:, :1] > k, gram[:, k : k + 1] / root, 0.0)
        gram = gram - below * head
        inverse = jnp.where(row == k, tail, inverse - below * tail)
    diag_ref[...] = diag[:8, :]
    block = block_ref[...].astype(jnp.float32)
    image = jnp.dot(
        inverse, block, precision=lax.Precision.HIGHEST, preferred_element_type=jnp.float32
    )
    out_ref[...] = (image * gain).astype(out_ref.dtype)


def factor(count, gram, block, dtype, gain=1.0):
    height = gram.shape[0]
    vmem = pl.BlockSpec(memory_space=pltpu.VMEM)
    image, diag = pl.pallas_call(
        functools.partial(factor_kernel, count, gain),
        in_specs=[vmem] * 2,
        out_specs=[vmem] * 2,
        out_shape=[
            jax.ShapeDtypeStruct(block.shape, dtype),
            jax.ShapeDtypeStruct((8, height), jnp.float32),
        ],
        name="factor",
    )(gram, block)
    return image, diag[0, :count]


def apply_tile(block, tile, transposed):
    side = 1 if transposed else 0
    product = lax.dot_general(
        block, tile, (((1,), (side,)), ((), ())), preferred_element_type=jnp.float32
    )
    return product.astype(jnp.bfloat16)


def local_gram(block):
    return lax.dot_general(
        block,
        block,
        (((1,), (1,)), ((), ())),
        precision=lax.Precision.HIGHEST,
        preferred_element_type=jnp.float32,
    )


def body(genotypes, snp_index, freq_table, prior, start_vectors):
    allele_freq = jnp.take(freq_table, snp_index)
    standard = standardize(genotypes, allele_freq).astype(jnp.bfloat16)
    samples = genotypes.shape[1]
    row_panel, col_panel = make_panels(standard)

    count = start_vectors.shape[1]
    height = -(-count // 32) * 32
    root = float(samples) ** 0.5
    start = jnp.pad((start_vectors / root).T, ((0, height - count), (0, 0))).astype(jnp.bfloat16)
    grm, tile, product = make_tile(row_panel, col_panel, start, prior)
    diagonals = []
    (image,) = axis_sum("row", 1, product)
    for step in range(1, ITERS):
        axis, ident = ("col", 2 * step) if step % 2 == 1 else ("row", 2 * step + 1)
        product, gram = axis_sum(
            axis, ident, apply_tile(image, tile, step % 2 == 1), local_gram(image)
        )
        last = step == ITERS - 1
        image, diag = factor(count, gram, product, jnp.float32 if last else jnp.bfloat16)
        diagonals.append(diag)
    (gram,) = axis_sum("col", 2 * ITERS, None, local_gram(image))
    image, diag = factor(count, gram, image, jnp.float32, root)
    diagonals.append(diag)
    return (grm, image[:count].T, jnp.stack(diagonals, axis=0))


def solution(mesh):
    return jax.shard_map(
        body,
        mesh=mesh,
        in_specs=(P(("row", "col"), None), P(("row", "col")), P(), P("row", "col"), P("row", None)),
        out_specs=(P("row", "col"), P("col", None), P()),
        check_vma=False,
    )
```

profile of v0, /device:TPU:0, one launch (start us, length us, event | category | flops | bytes accessed | tf_op | source)
XLA Modules:
  0.0 199.9 jit_solution(14211647378777700150)
XLA Ops:
  2.7 0.9 fusion
  3.6 0.7 pad.5.start_ref
  4.3 2.2 %divide_convert_fusion.std_ref = bf16[16,16384]{1,0:T(8,128)(2,1)} fusion(s32[16,16384]{1,0:T(8,128)} %param.5, f32[16]{0:T(128)S(1)} %multiply_sqrt_fusion, f32[16]{0:T(128)S(1)} %get-tuple-element.33), kind=kLoop, calls=%fused_computation.3 | loop fusion | flops 1048576 | bytes 1572992 | tf_op jit(solution)/shard_map/convert_element_type | solution.py:354
  6.5 62.2 %panels.1 = (bf16[8,4,16,2048]{3,2,1,0:T(8,128)(2,1)}, bf16[8,4,16,4096]{3,2,1,0:T(8,128)(2,1)}) custom-call(bf16[16,16384]{1,0:T(8,128)(2,1)} %divide_convert_fusion.std_ref), custom_call_target="tpu_custom_call" | custom-call | tf_op jit(solution)/shard_map/panels/pallas_call | solution.py:128
  68.7 33.4 %tile.1 = (f32[2048,4096]{1,0:T(8,128)}, bf16[2048,4096]{1,0:T(8,128)(2,1)}, bf16[32,4096]{1,0:T(8,128)(2,1)}) custom-call(bf16[512,2048]{1,0:T(8,128)(2,1)} %bitcast.38, bf16[512,4096]{1,0:T(8,128)(2,1)} %bitcast.37, bf16[32,2048]{1,0:T(8,128)(2,1)} %pad.5.start_ref, f32[2048,4096]{1,0:T(8,128)} %prior_ref.1), custom_call_target="tpu_custom_call" | custom-call | flops 8589934592 | bytes 83886080 | tf_op jit(solution)/shard_map/tile/pallas_call | solution.py:169
  102.1 1.7 copy.18
  103.8 15.5 %sum1.1 = bf16[32,4096]{1,0:T(8,128)(2,1)} custom-call(bf16[8,32,512]{2,1,0:T(8,128)(2,1)} %bitcast.41), custom_call_target="tpu_custom_call" | custom-call | tf_op jit(solution)/shard_map/sum1/pallas_call | solution.py:283
  119.3 1.8 fusion.1.refs_1_
  121.1 10.9 %convolution_convert_fusion.1 = bf16[32,2048]{1,0:T(8,128)(2,1)S(1)} fusion(bf16[32,4096]{1,0:T(8,128)(2,1)} %sum1.1, bf16[2048,4096]{1,0:T(8,128)(2,1)} %get-tuple-element.22), kind=kOutput, calls=%fused_computation.2 | convolution fusion | flops 536936448 | bytes 17170432 | tf_op jit(solution)/shard_map/dot_general | solution.py:336
  132.0 0.7 copy.19
  132.7 12.0 %sum2.1 = (bf16[32,2048]{1,0:T(8,128)(2,1)}, f32[32,32]{1,0:T(8,128)}) custom-call(bf16[4,32,512]{2,1,0:T(8,128)(2,1)} %bitcast.43, f32[32,32]{1,0:T(8,128)} %fusion.1.refs_1_), custom_call_target="tpu_custom_call" | custom-call | tf_op jit(solution)/shard_map/sum2/pallas_call | solution.py:283
  144.7 3.9 %factor.3 = (bf16[32,2048]{1,0:T(8,128)(2,1)}, f32[8,32]{1,0:T(8,128)}) custom-call(f32[32,32]{1,0:T(8,128)} %get-tuple-element.23.gram_ref, bf16[32,2048]{1,0:T(8,128)(2,1)} %get-tuple-element.24.block_ref), custom_call_target="tpu_custom_call" | custom-call | tf_op jit(solution)/shard_map/factor/pallas_call | solution.py:321
  148.6 8.9 %convolution_convert_fusion = bf16[32,4096]{1,0:T(8,128)(2,1)S(1)} fusion(bf16[32,2048]{1,0:T(8,128)(2,1)} %get-tuple-element.25, bf16[2048,4096]{1,0:T(8,128)(2,1)} %get-tuple-element.22), kind=kOutput, calls=%fused_computation.1 | convolution fusion | flops 537001984 | bytes 17170432 | tf_op jit(solution)/shard_map/dot_general | solution.py:336
  157.4 0.7 slice.13
  158.1 0.7 copy.17
  158.8 0.8 fusion.2.refs_1_
  159.6 19.6 %sum5.1 = (bf16[32,4096]{1,0:T(8,128)(2,1)}, f32[32,32]{1,0:T(8,128)}) custom-call(bf16[8,32,512]{2,1,0:T(8,128)(2,1)} %bitcast.40, f32[32,32]{1,0:T(8,128)} %fusion.2.refs_1_), custom_call_target="tpu_custom_call" | custom-call | tf_op jit(solution)/shard_map/sum5/pallas_call | solution.py:283
  179.2 4.2 %factor.4 = (f32[32,4096]{1,0:T(8,128)}, f32[8,32]{1,0:T(8,128)}) custom-call(f32[32,32]{1,0:T(8,128)} %get-tuple-element.26.gram_ref, bf16[32,4096]{1,0:T(8,128)(2,1)} %get-tuple-element.27.block_ref), custom_call_target="tpu_custom_call" | custom-call | tf_op jit(solution)/shard_map/factor/pallas_call | solution.py:321
  183.4 0.7 slice.14
  184.1 2.4 %fusion.3.refs_0_ = f32[32,32]{1,0:T(8,128)} fusion(f32[32,4096]{1,0:T(8,128)} %get-tuple-element.28.block_ref), kind=kOutput, calls=%fused_computation.18 | convolution fusion | flops 50331648 | bytes 528384 | tf_op jit(solution)/shard_map/dot_general | solution.py:343
  186.5 6.0 %sum6.1.gram_ref = f32[32,32]{1,0:T(8,128)} custom-call(f32[32,32]{1,0:T(8,128)} %fusion.3.refs_0_), custom_call_target="tpu_custom_call" | custom-call | tf_op jit(solution)/shard_map/sum6/pallas_call | solution.py:283
  192.5 4.3 %factor.5 = (f32[32,4096]{1,0:T(8,128)}, f32[8,32]{1,0:T(8,128)}) custom-call(f32[32,32]{1,0:T(8,128)} %sum6.1.gram_ref, f32[32,4096]{1,0:T(8,128)} %get-tuple-element.28.block_ref), custom_call_target="tpu_custom_call" | custom-call | tf_op jit(solution)/shard_map/factor/pallas_call | solution.py:321
  196.9 1.8 slice_bitcast_fusion
  198.6 0.7 slice.15
  (12 shorter events, 2.6 us)
Async XLA Ops:
  0.6 0.7 copy-start
  121.1 78.8 %copy-start.1 = (f32[2048]{0:T(1024)S(1)}, f32[2048]{0:T(1024)}, u32[]{:S(2)}) copy-start(f32[2048]{0:T(1024)} %param.7) | copy-start | bytes 24580
  148.6 10.3 %copy-start.2 = (bf16[32,2048]{1,0:T(8,128)(2,1)S(1)}, bf16[32,2048]{1,0:T(8,128)(2,1)}, u32[]{:S(2)}) copy-start(bf16[32,2048]{1,0:T(8,128)(2,1)} %get-tuple-element.25) | copy-start | bytes 393220
where the time goes:
time: 201 us; the launch traced here: 200 us
  Pallas kernels  161 us (80%)
  matrix products  24.7 us (12%)
  local copies, waits for them, and re-layouts  8.27 us (4%)
  other arithmetic  5.08 us (3%)
    pallas_call x1, Pallas kernels, make_panels(): pl.pallas_call(functools.partial(panel_kernel, nr, nc), in_specs=[vmem],...  62.2 us
    pallas_call x4, Pallas kernels, axis_sum(): pl.pallas_call(functools.partial(sum_kernel, axis, n, block is not None,...  53.1 us
    pallas_call x1, Pallas kernels, make_tile(): pl.pallas_call(functools.partial(tile_kernel, 1.0 / depth, min(512, rows)...  33.4 us
    dot_general x2, matrix products, apply_tile(): lax.dot_general(block, tile, (((1,), (side,)), ((), ())), preferred_eleme...  19.8 us
    pallas_call x3, Pallas kernels, factor(): pl.pallas_call(functools.partial(factor_kernel, count, gain), in_specs=[v...  12.4 us
    dot_general x3, matrix products, local_gram(): lax.dot_general(block, block, (((1,), (1,)), ((), ())), precision=lax.Pre...  4.98 us

commit v1 on v0

v1 whole, which is shorter than its diff:
```python
import functools

import jax
import jax.numpy as jnp
from jax import lax
from jax.experimental import pallas as pl
from jax.experimental.pallas import tpu as pltpu
from jax.sharding import PartitionSpec as P

ITERS = 3
MESH = pl.DeviceIdType.MESH
SLOTS = 4
F32, BF16 = jnp.float32, jnp.bfloat16


def dot(a, b, dims=((1,), (0,)), precision=None):
    return lax.dot_general(
        a, b, (dims, ((), ())), precision=precision, preferred_element_type=jnp.float32
    )


ROWS = ((1,), (1,))


def loop(size, step, body):
    step = min(step, size)

    def one(j, carry):
        body(pl.ds(pl.multiple_of(j * step, step), step))
        return carry

    lax.fori_loop(0, size // step, one, 0)


def cholesky_inverse(gram, count):
    height = gram.shape[0]
    row = lax.broadcasted_iota(jnp.int32, (height, 128), 0)
    lane = lax.broadcasted_iota(jnp.int32, (height, 128), 1)
    eye = jnp.where(row == lane - height, 1.0, 0.0).astype(F32)
    both = jnp.concatenate([gram, jnp.zeros((height, 128 - height), F32)], axis=1) + eye
    diag = jnp.zeros((1, 128), F32)
    for k in range(count):
        pivot = both[k : k + 1, k : k + 1]
        inv = lax.rsqrt(pivot)
        head = both[k : k + 1, :] * inv
        below = jnp.where(row[:, :1] > k, both[:, k : k + 1] * inv, 0.0)
        both = jnp.where(row == k, head, both - below * head)
        diag = jnp.where(lane[:1, :] == k, pivot * inv, diag)
    return both[:, height : 2 * height], diag


def main_kernel(nr, nc, count, root, *refs):
    idx, freq, geno, start, prior, rp_out, cp_out, tile_out, pcs, spectrum = refs[:10]
    refs = refs[10:]
    rp, cp, std, tile, stage, acc, vec, image = refs[:8]
    stage_sem, out_sem = refs[8:10]
    s_row, r_row, s_col, r_col, s_acr, r_acr, s_rt, r_rt, s_lt, r_lt = refs[10:20]
    sums_a, sums_b = refs[20:34], refs[34:48]
    cs_land, s_cs, r_cs = refs[48:51]
    grams = refs[51:]

    row, col = lax.axis_index("row"), lax.axis_index("col")
    own, samples = std.shape
    depth, lr = rp.shape
    lc = cp.shape[1]
    height = vec.shape[0]
    nz = nr // 2
    core, zed = lax.rem(row, 2), lax.div(row, 2)
    scale = 1.0 / depth
    row_peers = [lax.rem(row + d, nr) for d in range(1, nr)]
    col_peers = [lax.rem(col + d, nc) for d in range(1, nc)]
    z_peers = [lax.rem(zed + d, nz) for d in range(1, nz)]
    partner = row + 1 - 2 * core

    barrier = pltpu.get_barrier_semaphore()
    for peer in row_peers:
        pl.semaphore_signal(barrier, inc=1, device_id={"row": peer}, device_id_type=MESH)
    for peer in col_peers:
        pl.semaphore_signal(barrier, inc=1, device_id={"col": peer}, device_id_type=MESH)

    def remote(src, dst, send_sem, recv_sem, target):
        return pltpu.make_async_remote_copy(
            src_ref=src,
            dst_ref=dst,
            send_sem=send_sem,
            recv_sem=recv_sem,
            device_id=target,
            device_id_type=MESH,
        )

    band = stage.shape[1]
    bands = lr // band

    def fetch(i):
        return pltpu.make_async_copy(
            prior.at[pl.ds(i * band, band)], stage.at[i % SLOTS], stage_sem.at[i % SLOTS]
        )

    for i in range(min(SLOTS, bands)):
        fetch(i).start()

    place = lax.broadcasted_iota(jnp.int32, (own, 1), 0)
    allele = jnp.zeros((own, 1), F32)
    for j in range(own):
        allele = jnp.where(place == j, freq[idx[j]], allele)
    doubled = 2.0 * allele
    spread = jnp.sqrt(doubled * (1.0 - allele))
    levels = [(float(g) - doubled) / spread for g in range(3)]

    def standardize(part):
        g = geno[:, part]
        value = jnp.where(g == 0, levels[0], jnp.where(g == 1, levels[1], levels[2]))
        std[:, part] = value.astype(BF16)

    loop(samples, 2048, standardize)
    vec[...] = jnp.concatenate(
        [start[...] * (1.0 / root), jnp.zeros((height - count, lr), F32)], axis=0
    ).astype(BF16)

    pl.semaphore_wait(barrier, nr + nc - 2)

    def cut(index, length):
        return std.at[:, pl.ds(pl.multiple_of(index * length, 128), length)]

    def piece(panel, r, q):
        return panel.at[pl.ds(pl.multiple_of((r * nc + q) * own, own), own)]

    by_col = [
        remote(cut(peer, lc), piece(cp, row, col), s_col.at[d], r_col.at[d], {"col": peer})
        for d, peer in enumerate(col_peers)
    ]
    for copy in by_col:
        copy.start()
    piece(cp, row, col)[...] = cut(col, lc)[...]
    piece(rp, row, col)[...] = cut(row, lr)[...]

    by_row = [
        remote(cut(peer, lr), piece(rp, row, col), s_row.at[d], r_row.at[d], {"row": peer})
        for d, peer in enumerate(row_peers)
    ]
    across = []
    for d, peer in enumerate(col_peers):
        for r in range(nr):
            part = piece(rp, r, col)
            across.append(
                remote(part, part, s_acr.at[d, r], r_acr.at[d, r], {"col": peer})
            )

    right, left = lax.rem(row + 1, nr), lax.rem(row + nr - 1, nr)
    groups = min(nc, 4)
    width = nc // groups

    def bundle(r, e):
        g = lax.rem(lax.div(col, width) - e + groups, groups)
        size = width * own
        return cp.at[pl.ds(pl.multiple_of((r * groups + g) * size, size), size)]

    def rightward(s, e):
        part = bundle(lax.rem(row - s + nr, nr), e)
        return remote(part, part, s_rt.at[s, e], r_rt.at[s, e], {"row": right})

    def leftward(s, e):
        part = bundle(lax.rem(row + s, nr), e)
        return remote(part, part, s_lt.at[s, e], r_lt.at[s, e], {"row": left})

    def sends(s):
        return (row >= s) & (row < nr - 1), (row + s < nr) & (row > 0)

    def start_chain(s, e):
        to_right, to_left = sends(s)

        @pl.when(to_right)
        def _():
            rightward(s, e).start()

        @pl.when(to_left)
        def _():
            leftward(s, e).start()

    def receive(s, e):
        @pl.when(row - 1 - s >= 0)
        def _():
            part = bundle(lax.rem(row - 1 - s + nr, nr), e)
            remote(part, part, s_rt.at[s, e], r_rt.at[s, e], {"row": right}).wait_recv()

        @pl.when(row + 1 + s < nr)
        def _():
            part = bundle(lax.rem(row + 1 + s, nr), e)
            remote(part, part, s_lt.at[s, e], r_lt.at[s, e], {"row": left}).wait_recv()

    def arrive(e):
        g = lax.rem(lax.div(col, width) - e + groups, groups)
        for w in range(width):
            back = lax.rem(col - (g * width + w) + nc, nc)

            @pl.when(back > 0)
            def _():
                d = lax.max(back - 1, 0)
                part = piece(cp, row, g * width + w)
                remote(part, part, s_col.at[d], r_col.at[d], {"col": col_peers[0]}).wait_recv()

    def absorb(i):
        def work():
            fetch(i).wait()
            tile[pl.ds(i * band, band), :] = stage[i % SLOTS].astype(BF16)
            if i + SLOTS < bands:
                fetch(i + SLOTS).start()

        return work

    keep_tile = pltpu.make_async_copy(tile, tile_out, out_sem.at[0])

    def begin(part):
        acc[:, part] = dot(vec[...], tile[:, part])

    chunk = min(512, lc)
    todo = [absorb(i) for i in range(bands)] + [keep_tile.start]
    todo += [functools.partial(begin, pl.ds(j * chunk, chunk)) for j in range(lc // chunk)]

    for s in range(nr - 1):
        for e in range(groups):
            if s == 0:
                arrive(e)
            else:
                receive(s - 1, e)
            start_chain(s, e)
            if s == 0 and e == groups - 1:
                for copy in by_row:
                    copy.start()
            if s == min(2, nr - 2) and e == groups - 1:
                for copy in by_row:
                    copy.wait_recv()
                for copy in across:
                    copy.start()
            if todo:
                todo.pop(0)()
    while todo:
        todo.pop(0)()
    for e in range(groups):
        receive(nr - 2, e)
    for copy in across:
        copy.wait_recv()
    keep_rp = pltpu.make_async_copy(rp, rp_out, out_sem.at[1])
    keep_cp = pltpu.make_async_copy(cp, cp_out, out_sem.at[2])
    keep_rp.start()
    keep_cp.start()

    started = []

    def row_sum(bufs, during=None):
        mine, theirs, chip, zbuf, total, land = bufs[:6]
        s_p, r_p, s_z, r_z, s_g, r_g, s_f, r_f = bufs[6:]
        length = mine.shape[3]
        for h in range(2):
            for j in range(nz):
                low = (h * nz + j) * length
                mine[h, j] = acc[:, low : low + length].astype(BF16)
        swap = remote(mine.at[1 - core], theirs, s_p.at[0], r_p.at[0], {"row": partner})
        swap.start()
        swap.wait_recv()
        scatter = []
        for d, peer in enumerate(z_peers):
            chip[d] = (mine[core, peer].astype(F32) + theirs[peer].astype(F32)).astype(BF16)
            scatter.append(
                remote(chip.at[d], zbuf.at[d], s_z.at[d], r_z.at[d], {"row": 2 * peer + core})
            )
            scatter[-1].start()
        result = mine[core, zed].astype(F32) + theirs[zed].astype(F32)
        if during is not None:
            during()
        for d, copy in enumerate(scatter):
            copy.wait_recv()
            result = result + zbuf[d].astype(F32)
        total[...] = result.astype(BF16)
        land[core, zed] = result.astype(BF16)
        spread_out, forward = [], []
        for d, peer in enumerate(z_peers):
            spread_out.append(
                remote(total, land.at[core, zed], s_g.at[d], r_g.at[d], {"row": 2 * peer + core})
            )
            spread_out[-1].start()
        forward.append(
            remote(total, land.at[core, zed], s_f.at[0], r_f.at[0], {"row": partner})
        )
        forward[-1].start()
        for d in range(nz - 1):
            source = lax.rem(zed - d - 1 + nz, nz)
            part = land.at[core, source]
            remote(part, part, s_g.at[d], r_g.at[d], {"row": partner}).wait_recv()
            forward.append(
                remote(part, part, s_f.at[d + 1], r_f.at[d + 1], {"row": partner})
            )
            forward[-1].start()
        for d in range(nz):
            part = land.at[1 - core, lax.rem(zed - d + nz, nz)]
            remote(part, part, s_f.at[d], r_f.at[d], {"row": partner}).wait_recv()
        for h in range(2):
            for j in range(nz):
                low = (h * nz + j) * length
                image[:, low : low + length] = land[h, j].astype(F32)
        started.extend([swap] + scatter + spread_out + forward)

    def gram_send(axis, value, bufs):
        slots, out, s_g, r_g = bufs
        me, peers = (row, row_peers) if axis == "row" else (col, col_peers)
        out[...] = value
        slots[me] = value
        copies = []
        for d, peer in enumerate(peers):
            copies.append(remote(out, slots.at[me], s_g.at[d], r_g.at[d], {axis: peer}))
            copies[-1].start()
        started.extend(copies)
        return copies

    def gram_take(copies, bufs):
        for copy in copies:
            copy.wait_recv()
        total = bufs[0][0]
        for j in range(1, bufs[0].shape[0]):
            total = total + bufs[0][j]
        return total

    def note(step, diag):
        spectrum[step : step + 1, :] = diag[:, :count]

    weight = (dot(vec[...], rp[...], ROWS) * scale).astype(BF16)

    def finish(part):
        acc[:, part] = acc[:, part] + dot(weight, cp[:, part])

    loop(lc, 512, finish)
    row_sum(sums_a)

    first = image[...].astype(BF16)
    copies = gram_send("col", dot(first, first, ROWS), grams[:4])
    weight = (dot(first, cp[...], ROWS) * scale).astype(BF16)

    def middle(part):
        value = dot(image[...].astype(BF16), tile[part, :], ROWS) + dot(weight, rp[:, part])
        cs_land[col, :, part] = value.astype(BF16)

    loop(lr, 256, middle)
    exchange = []
    for d, peer in enumerate(col_peers):
        exchange.append(
            remote(cs_land.at[col], cs_land.at[col], s_cs.at[d], r_cs.at[d], {"col": peer})
        )
        exchange[-1].start()
    started.extend(exchange)
    inverse, diag = cholesky_inverse(gram_take(copies, grams[:4]), count)
    note(0, diag)
    for copy in exchange:
        copy.wait_recv()

    def normalize(part):
        block = cs_land[0, :, part].astype(F32)
        for j in range(1, nc):
            block = block + cs_land[j, :, part].astype(F32)
        vec[:, part] = dot(inverse, block, precision=lax.Precision.HIGHEST).astype(BF16)

    loop(lr, 512, normalize)

    second = vec[...]
    copies = gram_send("row", dot(second, second, ROWS), grams[4:8])
    weight = (dot(second, rp[...], ROWS) * scale).astype(BF16)

    def final(part):
        acc[:, part] = dot(vec[...], tile[:, part]) + dot(weight, cp[:, part])

    loop(lc, 512, final)
    kept = []

    def factor_second():
        kept.extend(cholesky_inverse(gram_take(copies, grams[4:8]), count))

    row_sum(sums_b, factor_second)
    inverse, diag = kept
    note(1, diag)

    def settle(part):
        acc[:, part] = dot(inverse, image[:, part], precision=lax.Precision.HIGHEST)

    loop(lc, 512, settle)
    third = acc[...].astype(BF16)
    copies = gram_send("col", dot(third, third, ROWS), grams[8:12])
    inverse, diag = cholesky_inverse(gram_take(copies, grams[8:12]), count)
    note(2, diag)
    inverse = inverse * root

    def emit(part):
        value = dot(inverse, acc[:, part], precision=lax.Precision.HIGHEST)
        pcs[:, part] = value[:count]

    loop(lc, 512, emit)

    for copy in by_col + by_row + across + started:
        copy.wait_send()
    for s in range(nr - 1):
        to_right, to_left = sends(s)
        for e in range(groups):

            @pl.when(to_right)
            def _():
                rightward(s, e).wait_send()

            @pl.when(to_left)
            def _():
                leftward(s, e).wait_send()

    keep_tile.wait()
    keep_rp.wait()
    keep_cp.wait()


def main_call(genotypes, snp_index, freq_table, prior, start):
    nr, nc = lax.axis_size("row"), lax.axis_size("col")
    own, samples = genotypes.shape
    depth = own * nr * nc
    lr, lc = prior.shape
    count = start.shape[0]
    height = -(-count // 32) * 32
    groups = min(nc, 4)
    nz = nr // 2
    length = lc // nr
    dma = pltpu.SemaphoreType.DMA
    vmem = pl.BlockSpec(memory_space=pltpu.VMEM)
    smem = pl.BlockSpec(memory_space=pltpu.SMEM)
    hbm = pl.BlockSpec(memory_space=pl.ANY)
    band = min(128, lr)

    def sum_scratch():
        return [
            pltpu.VMEM((2, nz, height, length), BF16),
            pltpu.VMEM((nz, height, length), BF16),
            pltpu.VMEM((nz - 1, height, length), BF16),
            pltpu.VMEM((nz - 1, height, length), BF16),
            pltpu.VMEM((height, length), BF16),
            pltpu.VMEM((2, nz, height, length), BF16),
            dma((1,)),
            dma((1,)),
            dma((nz - 1,)),
            dma((nz - 1,)),
            dma((nz - 1,)),
            dma((nz - 1,)),
            dma((nz,)),
            dma((nz,)),
        ]

    def gram_scratch(n):
        return [
            pltpu.VMEM((n, height, height), F32),
            pltpu.VMEM((height, height), F32),
            dma((n - 1,)),
            dma((n - 1,)),
        ]

    scratch = [
        pltpu.VMEM((depth, lr), BF16),
        pltpu.VMEM((depth, lc), BF16),
        pltpu.VMEM((own, samples), BF16),
        pltpu.VMEM((lr, lc), BF16),
        pltpu.VMEM((SLOTS, band, lc), F32),
        pltpu.VMEM((height, lc), F32),
        pltpu.VMEM((height, lr), BF16),
        pltpu.VMEM((height, lc), F32),
        dma((SLOTS,)),
        dma((3,)),
        dma((nr - 1,)),
        dma((nr - 1,)),
        dma((nc - 1,)),
        dma((nc - 1,)),
        dma((nc - 1, nr)),
        dma((nc - 1, nr)),
    ]
    scratch += [dma((nr - 1, groups))] * 4
    scratch += sum_scratch() + sum_scratch()
    scratch += [pltpu.VMEM((nc, height, lr), BF16), dma((nc - 1,)), dma((nc - 1,))]
    scratch += gram_scratch(nc) + gram_scratch(nr) + gram_scratch(nc)
    return pl.pallas_call(
        functools.partial(main_kernel, nr, nc, count, float(samples) ** 0.5),
        in_specs=[smem, smem, vmem, vmem, hbm],
        out_specs=[hbm, hbm, hbm, vmem, vmem],
        out_shape=[
            jax.ShapeDtypeStruct((depth, lr), BF16),
            jax.ShapeDtypeStruct((depth, lc), BF16),
            jax.ShapeDtypeStruct((lr, lc), BF16),
            jax.ShapeDtypeStruct((count, lc), F32),
            jax.ShapeDtypeStruct((ITERS, count), F32),
        ],
        scratch_shapes=scratch,
        compiler_params=pltpu.CompilerParams(
            collective_id=20, has_side_effects=True, vmem_limit_bytes=60 * 2**20
        ),
        name="main",
    )(snp_index, freq_table, genotypes, start, prior)


def tile_kernel(scale, rows_ref, cols_ref, prior_ref, grm_ref):
    def part(cut):
        window = dot(rows_ref[...], cols_ref[:, cut], ((0,), (0,)))
        grm_ref[:, cut] = prior_ref[:, cut].astype(F32) + window * scale

    step = min(512, cols_ref.shape[1])
    for low in range(0, cols_ref.shape[1], step):
        part(slice(low, low + step))


def make_tile(row_panel, col_panel, prior):
    depth = row_panel.shape[0]
    rows, cols = prior.shape
    bm = min(256, rows)
    return pl.pallas_call(
        functools.partial(tile_kernel, 1.0 / depth),
        grid=(rows // bm,),
        in_specs=[
            pl.BlockSpec((depth, bm), lambda i: (0, i)),
            pl.BlockSpec((depth, cols), lambda i: (0, 0)),
            pl.BlockSpec((bm, cols), lambda i: (i, 0)),
        ],
        out_specs=pl.BlockSpec((bm, cols), lambda i: (i, 0)),
        out_shape=jax.ShapeDtypeStruct((rows, cols), F32),
        compiler_params=pltpu.CompilerParams(
            dimension_semantics=("arbitrary",), vmem_limit_bytes=56 * 2**20
        ),
        cost_estimate=pl.CostEstimate(
            flops=2 * rows * cols * depth, bytes_accessed=6 * rows * cols, transcendentals=0
        ),
        name="tile",
    )(row_panel, col_panel, prior)


def body(genotypes, snp_index, freq_table, prior, start_vectors):
    row_panel, col_panel, tile, pcs, spectrum = main_call(
        genotypes, snp_index, freq_table, prior, start_vectors.T
    )
    return make_tile(row_panel, col_panel, tile), pcs.T, spectrum


def solution(mesh):
    return jax.shard_map(
        body,
        mesh=mesh,
        in_specs=(P(("row", "col"), None), P(("row", "col")), P(), P("row", "col"), P("row", None)),
        out_specs=(P("row", "col"), P("col", None), P()),
        check_vma=False,
    )
```

time: 201 us -> 140 us (0.70)
  matrix products: 24.7 us -> 0 us
  Pallas kernels: 161 us -> 138 us
  local copies, waits for them, and re-layouts: 8.27 us -> 1.33 us
  other arithmetic: 5.08 us -> 0 us
    dot_general x5 -> x0, matrix products: 24.7 us -> none  [the longest x2 19.8 us: apply_tile(): lax.dot_general(block, tile, (((1,), (side,)), ((), ())), preferred_eleme...]
    pallas_call x9 -> x2, Pallas kernels: 161 us -> 138 us  [the longest x1 115 us: main_call(): pl.pallas_call(functools.partial(main_kernel, nr, nc, count, float(sample...]
    reshape x3 -> x0, local copies, waits for them, and re-layouts: 3.08 us -> none  [axis_sum(): args.append(block.reshape(height, n, length).transpose(1, 0, 2))]
    convert_element_type x1 -> x0, other arithmetic: 2.2 us -> none  [body(): standard = standardize(genotypes, allele_freq).astype(jnp.bfloat16)]
    slice x3 -> x0, local copies, waits for them, and re-layouts: 2.07 us -> none  [factor(): return (image, diag[0, :count])]
where the time goes in v1:
time: 140 us
  Pallas kernels  138 us (99%)
    pallas_call x1, Pallas kernels, main_call(): pl.pallas_call(functools.partial(main_kernel, nr, nc, count, float(sample...  115 us
    pallas_call x1, Pallas kernels, make_tile(): pl.pallas_call(functools.partial(tile_kernel, 1.0 / depth), grid=(rows //...  22.7 us

profile of v1, /device:TPU:0, one launch (start us, length us, event | category | flops | bytes accessed | tf_op | source)
XLA Modules:
  0.0 139.5 jit_solution(13869163023684496098)
XLA Ops:
  0.6 114.9 %main.1 = (bf16[512,2048]{1,0:T(8,128)(2,1)}, bf16[512,4096]{1,0:T(8,128)(2,1)}, bf16[2048,4096]{1,0:T(8,128)(2,1)}, f32[20,4096]{1,0:T(8,128)}, f32[3,20]{1,0:T(4,128)}) custom-call(s32[16]{0:T(128)} %refs_0_.1, f32[2048]{0:T(1024)} %refs_1_.1, s32[16,16384]{1,0:T(8,128)} %refs_2_.1, f32[20,2048]{1,0:T(8,128)} %bitcast.3, f32[2048,4096]{1,0:T(8,128)} %refs_4_.1), custom_call_target="tpu_custom_call" | custom-call | tf_op jit(solution)/shard_map/main/pallas_call | solution.py:479
  115.5 0.0 copy-start
  115.5 0.0 copy-start.1
  115.5 22.7 %tile.1 = f32[2048,4096]{1,0:T(8,128)} custom-call(bf16[512,2048]{1,0:T(8,128)(2,1)} %get-tuple-element.8.rows_ref, bf16[512,4096]{1,0:T(8,128)(2,1)} %get-tuple-element.9.cols_ref, bf16[2048,4096]{1,0:T(8,128)(2,1)} %get-tuple-element.10.prior_ref), custom_call_target="tpu_custom_call" | custom-call | flops 8589934592 | bytes 50331648 | tf_op jit(solution)/shard_map/tile/pallas_call | solution.py:512
  138.2 0.0 copy-done
  138.2 0.7 copy.10
  139.0 0.0 copy-done.1
  139.0 0.6 copy.11
Async XLA Ops:
  115.5 22.7 %copy-start = (f32[20,4096]{1,0:T(8,128)S(1)}, f32[20,4096]{1,0:T(8,128)}, u32[]{:S(2)}) copy-start(f32[20,4096]{1,0:T(8,128)} %get-tuple-element.11) | copy-start | bytes 983044
  115.5 23.4 %copy-start.1 = (f32[3,20]{1,0:T(4,128)S(1)}, f32[3,20]{1,0:T(4,128)}, u32[]{:S(2)}) copy-start(f32[3,20]{1,0:T(4,128)} %get-tuple-element.18) | copy-start | bytes 724

commit v2 on v1

--- a/solution.py
+++ b/solution.py
@@ -10,6 +10,7 @@
 ITERS = 3
 MESH = pl.DeviceIdType.MESH
 SLOTS = 4
+HEIGHT = 8
 F32, BF16 = jnp.float32, jnp.bfloat16
 
 
@@ -30,6 +31,11 @@
         return carry
 
     lax.fori_loop(0, size // step, one, 0)
+
+
+def swung(q, e):
+    high, low = lax.div(q, 2) + e // 2, lax.rem(q, 2) + e % 2
+    return 2 * lax.rem(high, 2) + lax.rem(low, 2)
 
 
 def cholesky_inverse(gram, count):
@@ -50,14 +56,17 @@
 
 
 def main_kernel(nr, nc, count, root, *refs):
-    idx, freq, geno, start, prior, rp_out, cp_out, tile_out, pcs, spectrum = refs[:10]
+    idx_hbm, freq_hbm, geno_hbm, start_hbm, prior, rp, cp, tile, pcs, spectrum = refs[:10]
     refs = refs[10:]
-    rp, cp, std, tile, stage, acc, vec, image = refs[:8]
-    stage_sem, out_sem = refs[8:10]
+    idx, freq, start, geno = refs[:4]
+    refs = refs[4:]
+    std, stage, acc, vec, image, begun, shares = refs[:7]
+    refs = (None,) + refs
+    stage_sem, load_sem = refs[8:10]
     s_row, r_row, s_col, r_col, s_acr, r_acr, s_rt, r_rt, s_lt, r_lt = refs[10:20]
     sums_a, sums_b = refs[20:34], refs[34:48]
-    cs_land, s_cs, r_cs = refs[48:51]
-    grams = refs[51:]
+    cs_land, s_cs, r_cs, s_sh, r_sh, s_dir, r_dir, s_hub, r_hub, s_fan, r_fan = refs[48:59]
+    grams = refs[59:]
 
     row, col = lax.axis_index("row"), lax.axis_index("col")
     own, samples = std.shape
@@ -68,10 +77,14 @@
     core, zed = lax.rem(row, 2), lax.div(row, 2)
     scale = 1.0 / depth
     row_peers = [lax.rem(row + d, nr) for d in range(1, nr)]
-    col_peers = [lax.rem(col + d, nc) for d in range(1, nc)]
+    col_peers = [swung(col, d) if nc == 4 else lax.rem(col + d, nc) for d in range(1, nc)]
     z_peers = [lax.rem(zed + d, nz) for d in range(1, nz)]
     partner = row + 1 - 2 * core
 
+    loads = []
+    for source, target in ((idx_hbm, idx), (freq_hbm, freq), (start_hbm, start), (geno_hbm, geno)):
+        loads.append(pltpu.make_async_copy(source, target, load_sem.at[len(loads)]))
+        loads[-1].start()
     barrier = pltpu.get_barrier_semaphore()
     for peer in row_peers:
         pl.semaphore_signal(barrier, inc=1, device_id={"row": peer}, device_id_type=MESH)
@@ -91,6 +104,11 @@
     band = stage.shape[1]
     bands = lr // band
 
+    ratio = lc // lr
+    hub = lax.div(row, ratio)
+    offset = pl.multiple_of(lax.rem(row, ratio) * lr, 128)
+    relayed = nc <= 4
+
     def fetch(i):
         return pltpu.make_async_copy(
             prior.at[pl.ds(i * band, band)], stage.at[i % SLOTS], stage_sem.at[i % SLOTS]
@@ -99,6 +117,8 @@
     for i in range(min(SLOTS, bands)):
         fetch(i).start()
 
+    loads[0].wait()
+    loads[1].wait()
     place = lax.broadcasted_iota(jnp.int32, (own, 1), 0)
     allele = jnp.zeros((own, 1), F32)
     for j in range(own):
@@ -112,7 +132,9 @@
         value = jnp.where(g == 0, levels[0], jnp.where(g == 1, levels[1], levels[2]))
         std[:, part] = value.astype(BF16)
 
+    loads[3].wait()
     loop(samples, 2048, standardize)
+    loads[2].wait()
     vec[...] = jnp.concatenate(
         [start[...] * (1.0 / root), jnp.zeros((height - count, lr), F32)], axis=0
     ).astype(BF16)
@@ -134,40 +156,64 @@
     piece(cp, row, col)[...] = cut(col, lc)[...]
     piece(rp, row, col)[...] = cut(row, lr)[...]
 
-    by_row = [
-        remote(cut(peer, lr), piece(rp, row, col), s_row.at[d], r_row.at[d], {"row": peer})
-        for d, peer in enumerate(row_peers)
-    ]
-    across = []
-    for d, peer in enumerate(col_peers):
-        for r in range(nr):
-            part = piece(rp, r, col)
-            across.append(
-                remote(part, part, s_acr.at[d, r], r_acr.at[d, r], {"col": peer})
+    by_row, across, direct = [], [], []
+    if relayed:
+        for d, peer in enumerate(col_peers):
+            direct.append(
+                remote(cut(row, lr), piece(rp, row, col), s_dir.at[d], r_dir.at[d], {"col": peer})
             )
+    else:
+        for d, peer in enumerate(row_peers):
+            by_row.append(
+                remote(cut(peer, lr), piece(rp, row, col), s_row.at[d], r_row.at[d], {"row": peer})
+            )
+        for d, peer in enumerate(col_peers):
+            for r in range(nr):
+                part = piece(rp, r, col)
+                across.append(
+                    remote(part, part, s_acr.at[d, r], r_acr.at[d, r], {"col": peer})
+                )
+
+    @pl.when(col == hub)
+    def _():
+        begun[lax.rem(row, ratio)] = vec[...]
 
     right, left = lax.rem(row + 1, nr), lax.rem(row + nr - 1, nr)
     groups = min(nc, 4)
     width = nc // groups
 
-    def bundle(r, e):
-        g = lax.rem(lax.div(col, width) - e + groups, groups)
+    def group(base, e):
+        mine = lax.div(base, width)
+        return swung(mine, e) if groups == 4 else lax.rem(mine - e + groups, groups)
+
+    def bundle(r, e, panel=None, base=None):
+        base = col if base is None else base
+        g = group(base, e)
         size = width * own
-        return cp.at[pl.ds(pl.multiple_of((r * groups + g) * size, size), size)]
+        part = pl.ds(pl.multiple_of((r * groups + g) * size, size), size)
+        return (cp if panel is None else panel).at[part]
+
+    def packet(r, e):
+        return begun.at[lax.rem(r, ratio)] if e == groups else bundle(r, e)
+
+    def wanted(r, e):
+        return lax.div(r, ratio) == col if e == groups else True
 
     def rightward(s, e):
-        part = bundle(lax.rem(row - s + nr, nr), e)
+        part = packet(lax.rem(row - s + nr, nr), e)
         return remote(part, part, s_rt.at[s, e], r_rt.at[s, e], {"row": right})
 
     def leftward(s, e):
-        part = bundle(lax.rem(row + s, nr), e)
+        part = packet(lax.rem(row + s, nr), e)
         return remote(part, part, s_lt.at[s, e], r_lt.at[s, e], {"row": left})
 
-    def sends(s):
-        return (row >= s) & (row < nr - 1), (row + s < nr) & (row > 0)
+    def sends(s, e):
+        to_right = (row >= s) & (row < nr - 1) & wanted(lax.rem(row - s + nr, nr), e)
+        to_left = (row + s < nr) & (row > 0) & wanted(lax.rem(row + s, nr), e)
+        return to_right, to_left
 
     def start_chain(s, e):
-        to_right, to_left = sends(s)
+        to_right, to_left = sends(s, e)
 
         @pl.when(to_right)
         def _():
@@ -178,18 +224,87 @@
             leftward(s, e).start()
 
     def receive(s, e):
-        @pl.when(row - 1 - s >= 0)
+        from_left = lax.rem(row - 1 - s + nr, nr)
+        from_right = lax.rem(row + 1 + s, nr)
+
+        @pl.when((row - 1 - s >= 0) & wanted(from_left, e))
         def _():
-            part = bundle(lax.rem(row - 1 - s + nr, nr), e)
+            part = packet(from_left, e)
             remote(part, part, s_rt.at[s, e], r_rt.at[s, e], {"row": right}).wait_recv()
 
-        @pl.when(row + 1 + s < nr)
+        @pl.when((row + 1 + s < nr) & wanted(from_right, e))
         def _():
-            part = bundle(lax.rem(row + 1 + s, nr), e)
+            part = packet(from_right, e)
             remote(part, part, s_lt.at[s, e], r_lt.at[s, e], {"row": left}).wait_recv()
 
+    def hand(s, e, act):
+        for way in range(2):
+            k = (s * groups + e) * 2 + way
+            r = lax.rem(row + 1 + s, nr) if way else lax.rem(row - 1 - s + nr, nr)
+            valid = (row + 1 + s < nr) if way else (row - 1 - s >= 0)
+            turn = k % (nc - 1)
+            middle = lax.rem(hub + 1 + turn, nc)
+            part = bundle(r, e, rp, hub)
+
+            def feed():
+                source = bundle(r, e).at[:, pl.ds(offset, lr)]
+                return remote(
+                    source, part, s_hub.at[s, e, way], r_hub.at[s, e, way], {"col": middle}
+                )
+
+            def fan(m):
+                target = lax.rem(hub + 1 + (turn + m) % (nc - 1), nc)
+                return remote(
+                    part, part, s_fan.at[s, e, way, m - 1], r_fan.at[s, e, way], {"col": target}
+                )
+
+            if act == "feed":
+
+                @pl.when(valid & (col == hub))
+                def _():
+                    feed().start()
+                    part[...] = bundle(r, e)[:, pl.ds(offset, lr)]
+
+            if act == "fan":
+
+                @pl.when(valid & (col == middle))
+                def _():
+                    feed().wait_recv()
+                    for m in range(1, nc - 1):
+                        fan(m).start()
+
+            if act == "land":
+
+                @pl.when(valid & (col != hub) & (col != middle))
+                def _():
+                    fan(1).wait_recv()
+
+            if act == "drain":
+
+                @pl.when(valid & (col == hub))
+                def _():
+                    feed().wait_send()
+
+                @pl.when(valid & (col == middle))
+                def _():
+                    for m in range(1, nc - 1):
+                        fan(m).wait_send()
+
+    def hand_all(act):
+        if relayed:
+            for s in range(nr - 1):
+                for e in range(groups):
+                    hand(s, e, act)
+
     def arrive(e):
-        g = lax.rem(lax.div(col, width) - e + groups, groups)
+        g = group(col, e)
+        if nc == 4:
+            if e > 0:
+                part = piece(cp, row, g)
+                remote(
+                    part, part, s_col.at[e - 1], r_col.at[e - 1], {"col": col_peers[0]}
+                ).wait_recv()
+            return
         for w in range(width):
             back = lax.rem(col - (g * width + w) + nc, nc)
 
@@ -207,43 +322,6 @@
                 fetch(i + SLOTS).start()
 
         return work
-
-    keep_tile = pltpu.make_async_copy(tile, tile_out, out_sem.at[0])
-
-    def begin(part):
-        acc[:, part] = dot(vec[...], tile[:, part])
-
-    chunk = min(512, lc)
-    todo = [absorb(i) for i in range(bands)] + [keep_tile.start]
-    todo += [functools.partial(begin, pl.ds(j * chunk, chunk)) for j in range(lc // chunk)]
-
-    for s in range(nr - 1):
-        for e in range(groups):
-            if s == 0:
-                arrive(e)
-            else:
-                receive(s - 1, e)
-            start_chain(s, e)
-            if s == 0 and e == groups - 1:
-                for copy in by_row:
-                    copy.start()
-            if s == min(2, nr - 2) and e == groups - 1:
-                for copy in by_row:
-                    copy.wait_recv()
-                for copy in across:
-                    copy.start()
-            if todo:
-                todo.pop(0)()
-    while todo:
-        todo.pop(0)()
-    for e in range(groups):
-        receive(nr - 2, e)
-    for copy in across:
-        copy.wait_recv()
-    keep_rp = pltpu.make_async_copy(rp, rp_out, out_sem.at[1])
-    keep_cp = pltpu.make_async_copy(cp, cp_out, out_sem.at[2])
-    keep_rp.start()
-    keep_cp.start()
 
     started = []
 
@@ -257,6 +335,7 @@
                 mine[h, j] = acc[:, low : low + length].astype(BF16)
         swap = remote(mine.at[1 - core], theirs, s_p.at[0], r_p.at[0], {"row": partner})
         swap.start()
+        yield
         swap.wait_recv()
         scatter = []
         for d, peer in enumerate(z_peers):
@@ -268,6 +347,7 @@
         result = mine[core, zed].astype(F32) + theirs[zed].astype(F32)
         if during is not None:
             during()
+        yield
         for d, copy in enumerate(scatter):
             copy.wait_recv()
             result = result + zbuf[d].astype(F32)
@@ -283,6 +363,7 @@
             remote(total, land.at[core, zed], s_f.at[0], r_f.at[0], {"row": partner})
         )
         forward[-1].start()
+        yield
         for d in range(nz - 1):
             source = lax.rem(zed - d - 1 + nz, nz)
             part = land.at[core, source]
@@ -291,6 +372,7 @@
                 remote(part, part, s_f.at[d + 1], r_f.at[d + 1], {"row": partner})
             )
             forward[-1].start()
+        yield
         for d in range(nz):
             part = land.at[1 - core, lax.rem(zed - d + nz, nz)]
             remote(part, part, s_f.at[d], r_f.at[d], {"row": partner}).wait_recv()
@@ -299,6 +381,80 @@
                 low = (h * nz + j) * length
                 image[:, low : low + length] = land[h, j].astype(F32)
         started.extend([swap] + scatter + spread_out + forward)
+
+    def begin(part):
+        acc[:, part] = dot(vec[...], tile[:, part])
+
+    chunk = min(512, lc)
+    todo = [absorb(i) for i in range(bands)]
+    todo += [functools.partial(begin, pl.ds(j * chunk, chunk)) for j in range(lc // chunk)]
+    todo = [todo[i : i + 2] for i in range(0, len(todo), 2)]
+    stages = row_sum(sums_a)
+    step_on = [lambda: next(stages, None)]
+    for gap in (1, 6, 6):
+        todo += [step_on] + [[]] * gap
+
+    for s in range(nr - 1):
+        for e in range(groups):
+            if s == 0:
+                arrive(e)
+            else:
+                receive(s - 1, e)
+            start_chain(s, e)
+            if relayed and s > 0:
+                hand(s - 1, e, "feed")
+            if relayed and s > 1:
+                hand(s - 2, e, "fan")
+            if todo:
+                for work in todo.pop(0):
+                    work()
+        if s > 0:
+            receive(s - 1, groups)
+        start_chain(s, groups)
+        if s == 0:
+            for copy in by_row + direct:
+                copy.start()
+        if s == min(2, nr - 2):
+            for copy in by_row:
+                copy.wait_recv()
+            for copy in across:
+                copy.start()
+    for e in range(groups + 1):
+        receive(nr - 2, e)
+        if relayed and e < groups:
+            hand(nr - 2, e, "feed")
+            hand(nr - 3, e, "fan")
+    while todo:
+        for work in todo.pop(0):
+            work()
+
+    for i in range(ratio):
+        part = dot(begun[i], cp[:, i * lr : (i + 1) * lr], ROWS)
+        share = part if i == 0 else share + part
+    shares[col] = share.astype(BF16)
+    swaps = []
+    for d, peer in enumerate(col_peers):
+        swaps.append(
+            remote(shares.at[col], shares.at[col], s_sh.at[d], r_sh.at[d], {"col": peer})
+        )
+        swaps[-1].start()
+    started.extend(swaps)
+    if relayed:
+        for e in range(groups):
+            hand(nr - 2, e, "fan")
+    for _ in stages:
+        pass
+    for copy in swaps:
+        copy.wait_recv()
+    share = shares[0].astype(F32)
+    for j in range(1, nc):
+        share = share + shares[j].astype(F32)
+    weight = (share * scale).astype(BF16)
+
+    def complete(part):
+        image[:, part] = image[:, part] + dot(weight, cp[:, part])
+
+    loop(lc, 512, complete)
 
     def gram_send(axis, value, bufs):
         slots, out, s_g, r_g = bufs
@@ -323,42 +479,41 @@
     def note(step, diag):
         spectrum[step : step + 1, :] = diag[:, :count]
 
-    weight = (dot(vec[...], rp[...], ROWS) * scale).astype(BF16)
-
-    def finish(part):
-        acc[:, part] = acc[:, part] + dot(weight, cp[:, part])
-
-    loop(lc, 512, finish)
-    row_sum(sums_a)
-
     first = image[...].astype(BF16)
     copies = gram_send("col", dot(first, first, ROWS), grams[:4])
     weight = (dot(first, cp[...], ROWS) * scale).astype(BF16)
 
+    parts = nc if lr % (128 * nc) == 0 else 1
+    span = lr // parts
+    exchange = []
+
     def middle(part):
-        value = dot(image[...].astype(BF16), tile[part, :], ROWS) + dot(weight, rp[:, part])
-        cs_land[col, :, part] = value.astype(BF16)
+        acc[:, part] = dot(first, tile[part, :], ROWS)
 
     loop(lr, 256, middle)
-    exchange = []
-    for d, peer in enumerate(col_peers):
-        exchange.append(
-            remote(cs_land.at[col], cs_land.at[col], s_cs.at[d], r_cs.at[d], {"col": peer})
-        )
-        exchange[-1].start()
+    hand_all("land")
+    for copy in direct + across:
+        copy.wait_recv()
+
+    for p in range(parts):
+        low = p * span
+        value = acc[:, low : low + span] + dot(weight, rp[:, low : low + span])
+        cs_land[p, col] = value.astype(BF16)
+        for d, peer in enumerate(col_peers):
+            mine = cs_land.at[p, col]
+            exchange.append(remote(mine, mine, s_cs.at[d, p], r_cs.at[d, p], {"col": peer}))
+            exchange[-1].start()
     started.extend(exchange)
     inverse, diag = cholesky_inverse(gram_take(copies, grams[:4]), count)
     note(0, diag)
-    for copy in exchange:
-        copy.wait_recv()
-
-    def normalize(part):
-        block = cs_land[0, :, part].astype(F32)
+    for p in range(parts):
+        for copy in exchange[p * (nc - 1) : (p + 1) * (nc - 1)]:
+            copy.wait_recv()
+        block = cs_land[p, 0].astype(F32)
         for j in range(1, nc):
-            block = block + cs_land[j, :, part].astype(F32)
-        vec[:, part] = dot(inverse, block, precision=lax.Precision.HIGHEST).astype(BF16)
-
-    loop(lr, 512, normalize)
+            block = block + cs_land[p, j].astype(F32)
+        value = dot(inverse, block, precision=lax.Precision.HIGHEST)
+        vec[:, p * span : (p + 1) * span] = value.astype(BF16)
 
     second = vec[...]
     copies = gram_send("row", dot(second, second, ROWS), grams[4:8])
@@ -373,7 +528,8 @@
     def factor_second():
         kept.extend(cholesky_inverse(gram_take(copies, grams[4:8]), count))
 
-    row_sum(sums_b, factor_second)
+    for _ in row_sum(sums_b, factor_second):
+        pass
     inverse, diag = kept
     note(1, diag)
 
@@ -393,11 +549,11 @@
 
     loop(lc, 512, emit)
 
-    for copy in by_col + by_row + across + started:
+    for copy in by_col + by_row + across + direct + started:
         copy.wait_send()
     for s in range(nr - 1):
-        to_right, to_left = sends(s)
-        for e in range(groups):
+        for e in range(groups + 1):
+            to_right, to_left = sends(s, e)
 
             @pl.when(to_right)
             def _():
@@ -407,9 +563,7 @@
             def _():
                 leftward(s, e).wait_send()
 
-    keep_tile.wait()
-    keep_rp.wait()
-    keep_cp.wait()
+    hand_all("drain")
 
 
 def main_call(genotypes, snp_index, freq_table, prior, start):
@@ -418,14 +572,13 @@
     depth = own * nr * nc
     lr, lc = prior.shape
     count = start.shape[0]
-    height = -(-count // 32) * 32
+    height = -(-count // HEIGHT) * HEIGHT
     groups = min(nc, 4)
     nz = nr // 2
     length = lc // nr
     dma = pltpu.SemaphoreType.DMA
     vmem = pl.BlockSpec(memory_space=pltpu.VMEM)
-    smem = pl.BlockSpec(memory_space=pltpu.SMEM)
-    hbm = pl.BlockSpec(memory_space=pl.ANY)
+    hbm = pl.BlockSpec(memory_space=pltpu.HBM)
     band = min(128, lr)
 
     def sum_scratch():
@@ -454,17 +607,21 @@
             dma((n - 1,)),
         ]
 
+    one = nr - 1 if nc <= 4 else 1
     scratch = [
-        pltpu.VMEM((depth, lr), BF16),
-        pltpu.VMEM((depth, lc), BF16),
+        pltpu.SMEM((own,), jnp.int32),
+        pltpu.SMEM(freq_table.shape, F32),
+        pltpu.VMEM((count, lr), F32),
+        pltpu.VMEM((own, samples), jnp.int32),
         pltpu.VMEM((own, samples), BF16),
-        pltpu.VMEM((lr, lc), BF16),
         pltpu.VMEM((SLOTS, band, lc), F32),
         pltpu.VMEM((height, lc), F32),
         pltpu.VMEM((height, lr), BF16),
         pltpu.VMEM((height, lc), F32),
+        pltpu.VMEM((lc // lr, height, lr), BF16),
+        pltpu.VMEM((nc, height, depth), BF16),
         dma((SLOTS,)),
-        dma((3,)),
+        dma((4,)),
         dma((nr - 1,)),
         dma((nr - 1,)),
         dma((nc - 1,)),
@@ -472,14 +629,19 @@
         dma((nc - 1, nr)),
         dma((nc - 1, nr)),
     ]
-    scratch += [dma((nr - 1, groups))] * 4
+    scratch += [dma((nr - 1, groups + 1))] * 4
     scratch += sum_scratch() + sum_scratch()
-    scratch += [pltpu.VMEM((nc, height, lr), BF16), dma((nc - 1,)), dma((nc - 1,))]
+    parts = nc if lr % (128 * nc) == 0 else 1
+    scratch += [pltpu.VMEM((parts, nc, height, lr // parts), BF16)]
+    scratch += [dma((nc - 1, parts))] * 2
+    scratch += [dma((nc - 1,))] * 4
+    scratch += [dma((one, groups, 2))] * 2 + [dma((one, groups, 2, nc - 2)), dma((one, groups, 2))]
     scratch += gram_scratch(nc) + gram_scratch(nr) + gram_scratch(nc)
+    args = (snp_index, freq_table, genotypes, start, prior)
     return pl.pallas_call(
         functools.partial(main_kernel, nr, nc, count, float(samples) ** 0.5),
-        in_specs=[smem, smem, vmem, vmem, hbm],
-        out_specs=[hbm, hbm, hbm, vmem, vmem],
+        in_specs=[hbm] * 5,
+        out_specs=[vmem] * 5,
         out_shape=[
             jax.ShapeDtypeStruct((depth, lr), BF16),
             jax.ShapeDtypeStruct((depth, lc), BF16),
@@ -489,13 +651,18 @@
         ],
         scratch_shapes=scratch,
         compiler_params=pltpu.CompilerParams(
-            collective_id=20, has_side_effects=True, vmem_limit_bytes=60 * 2**20
+            collective_id=20, has_side_effects=True, vmem_limit_bytes=22 * 2**20
         ),
         name="main",
-    )(snp_index, freq_table, genotypes, start, prior)
-
-
-def tile_kernel(scale, rows_ref, cols_ref, prior_ref, grm_ref):
+    )(*[pltpu.with_memory_space_constraint(x, pltpu.HBM) for x in args])
+
+
+def tile_kernel(scale, rows_ref, cols_ref, prior_ref, pcs_ref, spectrum_ref, grm_ref, v_ref, d_ref):
+    @pl.when(pl.program_id(0) == 0)
+    def _():
+        v_ref[...] = pcs_ref[...]
+        d_ref[...] = spectrum_ref[...]
+
     def part(cut):
         window = dot(rows_ref[...], cols_ref[:, cut], ((0,), (0,)))
         grm_ref[:, cut] = prior_ref[:, cut].astype(F32) + window * scale
@@ -505,7 +672,7 @@
         part(slice(low, low + step))
 
 
-def make_tile(row_panel, col_panel, prior):
+def make_tile(row_panel, col_panel, prior, pcs, spectrum):
     depth = row_panel.shape[0]
     rows, cols = prior.shape
     bm = min(256, rows)
@@ -516,24 +683,35 @@
             pl.BlockSpec((depth, bm), lambda i: (0, i)),
             pl.BlockSpec((depth, cols), lambda i: (0, 0)),
             pl.BlockSpec((bm, cols), lambda i: (i, 0)),
+            pl.BlockSpec(pcs.shape, lambda i: (0, 0)),
+            pl.BlockSpec(spectrum.shape, lambda i: (0, 0)),
         ],
-        out_specs=pl.BlockSpec((bm, cols), lambda i: (i, 0)),
-        out_shape=jax.ShapeDtypeStruct((rows, cols), F32),
+        out_specs=[
+            pl.BlockSpec((bm, cols), lambda i: (i, 0)),
+            pl.BlockSpec(pcs.shape, lambda i: (0, 0)),
+            pl.BlockSpec(spectrum.shape, lambda i: (0, 0)),
+        ],
+        out_shape=[
+            jax.ShapeDtypeStruct((rows, cols), F32),
+            jax.ShapeDtypeStruct(pcs.shape, F32),
+            jax.ShapeDtypeStruct(spectrum.shape, F32),
+        ],
         compiler_params=pltpu.CompilerParams(
-            dimension_semantics=("arbitrary",), vmem_limit_bytes=56 * 2**20
+            dimension_semantics=("arbitrary",), vmem_limit_bytes=24 * 2**20
         ),
         cost_estimate=pl.CostEstimate(
             flops=2 * rows * cols * depth, bytes_accessed=6 * rows * cols, transcendentals=0
         ),
         name="tile",
-    )(row_panel, col_panel, prior)
+    )(row_panel, col_panel, prior, pcs, spectrum)
 
 
 def body(genotypes, snp_index, freq_table, prior, start_vectors):
     row_panel, col_panel, tile, pcs, spectrum = main_call(
         genotypes, snp_index, freq_table, prior, start_vectors.T
     )
-    return make_tile(row_panel, col_panel, tile), pcs.T, spectrum
+    grm, pcs, spectrum = make_tile(row_panel, col_panel, tile, pcs, spectrum)
+    return grm, pcs.T, spectrum
 
 
 def solution(mesh):

time: 140 us -> 120 us (0.86)
  Pallas kernels: 138 us -> 119 us
    pallas_call x1, Pallas kernels: 115 us -> 104 us  [main_call(): pl.pallas_call(functools.partial(main_kernel, nr, nc, count, float(sample...]
    pallas_call x1, Pallas kernels: 22.7 us -> 15 us  [make_tile(): pl.pallas_call(functools.partial(tile_kernel, 1.0 / depth), grid=(rows //...]
where the time goes in v2:
time: 120 us
  Pallas kernels  119 us (99%)
    pallas_call x1, Pallas kernels, main_call(): pl.pallas_call(functools.partial(main_kernel, nr, nc, count, float(sample...  104 us
    pallas_call x1, Pallas kernels, make_tile(): pl.pallas_call(functools.partial(tile_kernel, 1.0 / depth), grid=(rows //...  15 us

profile of v2, /device:TPU:0, one launch (start us, length us, event | category | flops | bytes accessed | tf_op | source)
XLA Modules:
  0.0 119.5 jit_solution(8750795474276799416)
XLA Ops:
  0.6 103.9 %main.1 = (bf16[512,2048]{1,0:T(8,128)(2,1)S(1)}, bf16[512,4096]{1,0:T(8,128)(2,1)S(1)}, bf16[2048,4096]{1,0:T(8,128)(2,1)S(1)}, f32[20,4096]{1,0:T(8,128)S(1)}, f32[3,20]{1,0:T(4,128)S(1)}) custom-call(s32[16]{0:T(128)} %refs_0_.1, f32[2048]{0:T(1024)} %refs_1_.1, s32[16,16384]{1,0:T(8,128)} %refs_2_.1, f32[20,2048]{1,0:T(8,128)} %bitcast.2, ...), custom_call_target="tpu_custom_call" | custom-call | tf_op jit(solution)/shard_map/main/pallas_call | solution.py:641
  104.6 15.0 %tile.1 = (f32[2048,4096]{1,0:T(8,128)}, f32[20,4096]{1,0:T(8,128)}, f32[3,20]{1,0:T(4,128)}) custom-call(bf16[512,2048]{1,0:T(8,128)(2,1)S(1)} %get-tuple-element.11.rows_ref, bf16[512,4096]{1,0:T(8,128)(2,1)S(1)} %get-tuple-element.12.cols_ref, bf16[2048,4096]{1,0:T(8,128)(2,1)S(1)} %get-tuple-element.13.prior_ref, ...), custom_call_target="tpu_custom_call" | custom-call | flops 8589934592 | bytes 50331648 | tf_op jit(solution)/shard_map/tile/pallas_call | solution.py:679

commit v3 on v2

--- a/solution.py
+++ b/solution.py
@@ -11,6 +11,7 @@
 MESH = pl.DeviceIdType.MESH
 SLOTS = 4
 HEIGHT = 8
+LAG = 2
 F32, BF16 = jnp.float32, jnp.bfloat16
 
 
@@ -325,26 +326,46 @@
 
     started = []
 
-    def row_sum(bufs, during=None):
+    def row_sum(bufs, during=None, make=None):
         mine, theirs, chip, zbuf, total, land = bufs[:6]
         s_p, r_p, s_z, r_z, s_g, r_g, s_f, r_f = bufs[6:]
         length = mine.shape[3]
-        for h in range(2):
-            for j in range(nz):
-                low = (h * nz + j) * length
-                mine[h, j] = acc[:, low : low + length].astype(BF16)
-        swap = remote(mine.at[1 - core], theirs, s_p.at[0], r_p.at[0], {"row": partner})
-        swap.start()
-        yield
-        swap.wait_recv()
-        scatter = []
-        for d, peer in enumerate(z_peers):
-            chip[d] = (mine[core, peer].astype(F32) + theirs[peer].astype(F32)).astype(BF16)
-            scatter.append(
-                remote(chip.at[d], zbuf.at[d], s_z.at[d], r_z.at[d], {"row": 2 * peer + core})
-            )
-            scatter[-1].start()
-        result = mine[core, zed].astype(F32) + theirs[zed].astype(F32)
+        swaps, scatter = [], []
+        if make is None:
+            for h in range(2):
+                for j in range(nz):
+                    low = (h * nz + j) * length
+                    mine[h, j] = acc[:, low : low + length].astype(BF16)
+            swaps.append(remote(mine.at[1 - core], theirs, s_p.at[0], r_p.at[0], {"row": partner}))
+            swaps[0].start()
+            yield
+            swaps[0].wait_recv()
+        else:
+            for t, z in enumerate(z_peers + [zed]):
+                mine[1 - core, z] = make((1 - core) * nz + z).astype(BF16)
+                swaps.append(
+                    remote(
+                        mine.at[1 - core, z],
+                        theirs.at[z],
+                        s_p.at[t],
+                        r_p.at[t],
+                        {"row": partner},
+                    )
+                )
+                swaps[-1].start()
+        for t, z in enumerate(z_peers + [zed]):
+            if make is None:
+                result = mine[core, z].astype(F32)
+            else:
+                result = make(core * nz + z)
+                swaps[t].wait_recv()
+            result = result + theirs[z].astype(F32)
+            if t < nz - 1:
+                chip[t] = result.astype(BF16)
+                scatter.append(
+                    remote(chip.at[t], zbuf.at[t], s_z.at[t], r_z.at[t], {"row": 2 * z + core})
+                )
+                scatter[-1].start()
         if during is not None:
             during()
         yield
@@ -376,11 +397,12 @@
         for d in range(nz):
             part = land.at[1 - core, lax.rem(zed - d + nz, nz)]
             remote(part, part, s_f.at[d], r_f.at[d], {"row": partner}).wait_recv()
-        for h in range(2):
-            for j in range(nz):
-                low = (h * nz + j) * length
-                image[:, low : low + length] = land[h, j].astype(F32)
-        started.extend([swap] + scatter + spread_out + forward)
+        if during is None:
+            for h in range(2):
+                for j in range(nz):
+                    low = (h * nz + j) * length
+                    image[:, low : low + length] = land[h, j].astype(F32)
+        started.extend(swaps + scatter + spread_out + forward)
 
     def begin(part):
         acc[:, part] = dot(vec[...], tile[:, part])
@@ -391,7 +413,7 @@
     todo = [todo[i : i + 2] for i in range(0, len(todo), 2)]
     stages = row_sum(sums_a)
     step_on = [lambda: next(stages, None)]
-    for gap in (1, 6, 6):
+    for gap in (1, 4, 5):
         todo += [step_on] + [[]] * gap
 
     for s in range(nr - 1):
@@ -403,8 +425,8 @@
             start_chain(s, e)
             if relayed and s > 0:
                 hand(s - 1, e, "feed")
-            if relayed and s > 1:
-                hand(s - 2, e, "fan")
+            if relayed and s >= LAG:
+                hand(s - LAG, e, "fan")
             if todo:
                 for work in todo.pop(0):
                     work()
@@ -423,7 +445,8 @@
         receive(nr - 2, e)
         if relayed and e < groups:
             hand(nr - 2, e, "feed")
-            hand(nr - 3, e, "fan")
+            for q in range(max(nr - 1 - LAG, 0), nr - 2):
+                hand(q, e, "fan")
     while todo:
         for work in todo.pop(0):
             work()
@@ -519,35 +542,47 @@
     copies = gram_send("row", dot(second, second, ROWS), grams[4:8])
     weight = (dot(second, rp[...], ROWS) * scale).astype(BF16)
 
-    def final(part):
-        acc[:, part] = dot(vec[...], tile[:, part]) + dot(weight, cp[:, part])
-
-    loop(lc, 512, final)
+    length = lc // nr
+    if length % 128 == 0:
+
+        def make(k):
+            part = pl.ds(pl.multiple_of(k * length, 128), length)
+            return dot(vec[...], tile[:, part]) + dot(weight, cp[:, part])
+
+    else:
+        make = None
+
+        def final(part):
+            acc[:, part] = dot(vec[...], tile[:, part]) + dot(weight, cp[:, part])
+
+        loop(lc, 512, final)
     kept = []
 
     def factor_second():
         kept.extend(cholesky_inverse(gram_take(copies, grams[4:8]), count))
 
-    for _ in row_sum(sums_b, factor_second):
+    for _ in row_sum(sums_b, factor_second, make):
         pass
     inverse, diag = kept
     note(1, diag)
-
-    def settle(part):
-        acc[:, part] = dot(inverse, image[:, part], precision=lax.Precision.HIGHEST)
-
-    loop(lc, 512, settle)
-    third = acc[...].astype(BF16)
-    copies = gram_send("col", dot(third, third, ROWS), grams[8:12])
-    inverse, diag = cholesky_inverse(gram_take(copies, grams[8:12]), count)
+    blocks = [(h, j) for h in range(2) for j in range(nz)]
+    ready = sums_b[5]
+    gram = jnp.zeros((height, height), F32)
+    for h, j in blocks:
+        gram = gram + dot(ready[h, j], ready[h, j], ROWS)
+    copies = gram_send("col", gram, grams[8:12])
+    exact = lax.Precision.HIGHEST
+    gram = dot(inverse, gram_take(copies, grams[8:12]), precision=exact)
+    gram = dot(gram, inverse, ROWS, precision=exact)
+    last, diag = cholesky_inverse(gram, count)
     note(2, diag)
-    inverse = inverse * root
-
-    def emit(part):
-        value = dot(inverse, acc[:, part], precision=lax.Precision.HIGHEST)
-        pcs[:, part] = value[:count]
-
-    loop(lc, 512, emit)
+    turn = dot(last, inverse, precision=exact) * root
+    coarse = turn.astype(BF16)
+    stack = jnp.concatenate([coarse, (turn - coarse.astype(F32)).astype(BF16)], axis=0)
+    for h, j in blocks:
+        low = (h * nz + j) * length
+        value = dot(stack, ready[h, j])
+        pcs[:, low : low + length] = (value[:height] + value[height:])[:count]
 
     for copy in by_col + by_row + across + direct + started:
         copy.wait_send()
@@ -589,8 +624,8 @@
             pltpu.VMEM((nz - 1, height, length), BF16),
             pltpu.VMEM((height, length), BF16),
             pltpu.VMEM((2, nz, height, length), BF16),
-            dma((1,)),
-            dma((1,)),
+            dma((nz,)),
+            dma((nz,)),
             dma((nz - 1,)),
             dma((nz - 1,)),
             dma((nz - 1,)),

time: 120 us -> 114 us (0.950)
  Pallas kernels: 119 us -> 113 us
    pallas_call x1, Pallas kernels: 104 us -> 98.4 us  [main_call(): pl.pallas_call(functools.partial(main_kernel, nr, nc, count, float(sample...]
where the time goes in v3:
time: 114 us
  Pallas kernels  113 us (99%)
    pallas_call x1, Pallas kernels, main_call(): pl.pallas_call(functools.partial(main_kernel, nr, nc, count, float(sample...  98.4 us
    pallas_call x1, Pallas kernels, make_tile(): pl.pallas_call(functools.partial(tile_kernel, 1.0 / depth), grid=(rows //...  15 us

profile of v3, /device:TPU:0, one launch (start us, length us, event | category | flops | bytes accessed | tf_op | source)
XLA Modules:
  0.0 114.1 jit_solution(4641033328083791133)
XLA Ops:
  0.6 98.4 %main.1 = (bf16[512,2048]{1,0:T(8,128)(2,1)S(1)}, bf16[512,4096]{1,0:T(8,128)(2,1)S(1)}, bf16[2048,4096]{1,0:T(8,128)(2,1)S(1)}, f32[20,4096]{1,0:T(8,128)S(1)}, f32[3,20]{1,0:T(4,128)S(1)}) custom-call(s32[16]{0:T(128)} %refs_0_.1, f32[2048]{0:T(1024)} %refs_1_.1, s32[16,16384]{1,0:T(8,128)} %refs_2_.1, f32[20,2048]{1,0:T(8,128)} %bitcast.2, ...), custom_call_target="tpu_custom_call" | custom-call | tf_op jit(solution)/shard_map/main/pallas_call | solution.py:676
  99.1 15.0 %tile.1 = (f32[2048,4096]{1,0:T(8,128)}, f32[20,4096]{1,0:T(8,128)}, f32[3,20]{1,0:T(4,128)}) custom-call(bf16[512,2048]{1,0:T(8,128)(2,1)S(1)} %get-tuple-element.11.rows_ref, bf16[512,4096]{1,0:T(8,128)(2,1)S(1)} %get-tuple-element.12.cols_ref, bf16[2048,4096]{1,0:T(8,128)(2,1)S(1)} %get-tuple-element.13.prior_ref, ...), custom_call_target="tpu_custom_call" | custom-call | flops 8589934592 | bytes 50331648 | tf_op jit(solution)/shard_map/tile/pallas_call | solution.py:714
